TPU v7x, 32 devices: a whole 2x2x4 slice. The times are simulated.
32 devices in a mesh: gx: 4 (over y, core), gy: 8 (over z, x).
Axes of the slice: x: 2, y: 2, z: 4, core: 2. Of those that a mesh axis runs over, the one named last changes fastest.
Arguments:
- wavefield: float32 [8, 16, 3, 125, 256], P('gx', 'gy'), may hold values from -0.6 to 0.6
- moduli: float32 [8, 16, 2, 256], P('gx', 'gy'), may hold values from 0.5 to 4
- residuals: float32 [32, 32, 128], P(('gx', 'gy')), may hold values from -6 to 6
- coords: float32 [32, 32, 3, 128], P(('gx', 'gy')), may hold values from -1 to 1
- angles: float32 [32, 32, 2, 128], P(('gx', 'gy')), may hold values from -3.140625 to 3.140625
- element_ids: int32 [32, 32, 128], P(('gx', 'gy')), may hold values from 0 to 1023
- counts: int32 [32, 32], P(('gx', 'gy')), may hold values from 0 to 128, as said below
Outputs:
- force: float32 [8, 16, 3, 125, 256], P('gx', 'gy')
Inputs may be any that keep to these rules, and one draw needn't show every extreme that they name: `counts`: each sending device has at least one tile with exactly 128 live slots; in every draw one owner receives 128 live slots from every sender. The lightest owners receive on average about a sixth of 128 a sender, the others lie between.
All inputs are finite; a program needn't handle non-finite values.
Results may differ from a plain program's by a relative error of at most 0.0003.
Values sent between devices are 32-bit elements; how exact they have to be, the bound alone decides.
A program may use at most 64 MiB of HBM per device.

v0:
```python
import math
import jax
import jax.numpy as jnp
import numpy as np
from jax import lax
from jax.sharding import PartitionSpec as P


def with_halo(block, sides, width):
    for axis, dim in sides:
        count = lax.axis_size(axis)
        forward = [(i, i + 1) for i in range(count - 1)]
        backward = [(target, source) for source, target in forward]
        low = lax.ppermute(
            lax.slice_in_dim(block, block.shape[dim] - width, None, axis=dim), axis, forward
        )
        high = lax.ppermute(lax.slice_in_dim(block, 0, width, axis=dim), axis, backward)
        block = jnp.concatenate([low, block, high], axis=dim)
    return block


def gll_points():
    return np.array([-1.0, -math.sqrt(3.0 / 7.0), 0.0, math.sqrt(3.0 / 7.0), 1.0])


def gll_weights():
    return np.array([0.1, 49.0 / 90.0, 32.0 / 45.0, 49.0 / 90.0, 0.1])


def derivative_table():
    points = gll_points()
    table = np.zeros((5, 5))
    for row in range(5):
        for col in range(5):
            if row == col:
                table[row, col] = sum(
                    (1.0 / (points[col] - points[other]) for other in range(5) if other != col)
                )
            else:
                value = 1.0 / (points[col] - points[row])
                for other in range(5):
                    if other != col and other != row:
                        value = (
                            value * (points[row] - points[other]) / (points[col] - points[other])
                        )
                table[row, col] = value
    return table


def basis(where):
    points = gll_points()
    values = []
    slopes = []
    for node in range(5):
        value = jnp.ones_like(where)
        slope = jnp.zeros_like(where)
        for other in range(5):
            if other != node:
                scale = 1.0 / (points[node] - points[other])
                factor = (where - points[other]) * scale
                slope = slope * factor + value * scale
                value = value * factor
        values.append(value)
        slopes.append(slope)
    return (jnp.stack(values), jnp.stack(slopes))


def sources(resid, coord, angle, live_count):
    slots = resid.shape[-1]
    live = jnp.arange(slots, dtype=jnp.int32)[None, :] < live_count[:, None]
    value = jnp.where(live, resid, 0.0).reshape(-1)
    first = coord[:, 0, :].reshape(-1)
    second = coord[:, 1, :].reshape(-1)
    third = coord[:, 2, :].reshape(-1)
    azimuth = angle[:, 0, :].reshape(-1)
    dip = angle[:, 1, :].reshape(-1)
    tang_x = jnp.cos(azimuth) * jnp.cos(dip)
    tang_y = jnp.sin(azimuth) * jnp.cos(dip)
    tang_z = jnp.sin(dip)
    val_x, der_x = basis(first)
    val_y, der_y = basis(second)
    val_z, der_z = basis(third)
    shape = (
        tang_x * der_x[:, None, None, :] * val_y[None, :, None, :] * val_z[None, None, :, :]
        + tang_y * val_x[:, None, None, :] * der_y[None, :, None, :] * val_z[None, None, :, :]
        + tang_z * val_x[:, None, None, :] * val_y[None, :, None, :] * der_z[None, None, :, :]
    )
    direction = jnp.stack([tang_x, tang_y, tang_z]) * value[None, :]
    return (direction[:, None, None, None, :] * shape[None]).reshape(375, -1)


def along(field, table, dim):
    if dim == 0:
        return jnp.einsum("pa,...aqsz->...pqsz", table, field, precision=lax.Precision.HIGHEST)
    if dim == 1:
        return jnp.einsum("qb,...pbsz->...pqsz", table, field, precision=lax.Precision.HIGHEST)
    return jnp.einsum("sc,...pqcz->...pqsz", table, field, precision=lax.Precision.HIGHEST)


def back(field, table, dim):
    if dim == 0:
        return jnp.einsum("pa,...pqsz->...aqsz", table, field, precision=lax.Precision.HIGHEST)
    if dim == 1:
        return jnp.einsum("qb,...pqsz->...pbsz", table, field, precision=lax.Precision.HIGHEST)
    return jnp.einsum("sc,...pqsz->...pqcz", table, field, precision=lax.Precision.HIGHEST)


def stiffness(field, moduli):
    table = jnp.asarray(derivative_table(), jnp.float32)
    weight = jnp.asarray(gll_weights(), jnp.float32)
    wgrid = (weight[:, None, None] * weight[None, :, None] * weight[None, None, :])[:, :, :, None]
    grads = [along(field, table, dim) for dim in range(3)]
    lame = moduli[..., 0, :][..., None, None, None, :]
    shear = moduli[..., 1, :][..., None, None, None, :]
    diverge = (
        grads[0][..., 0, :, :, :, :] + grads[1][..., 1, :, :, :, :] + grads[2][..., 2, :, :, :, :]
    )
    result = jnp.zeros_like(field)
    for col in range(3):
        parts = []
        for row in range(3):
            stress = shear * (grads[col][..., row, :, :, :, :] + grads[row][..., col, :, :, :, :])
            if row == col:
                stress = stress + lame * diverge
            parts.append(stress * wgrid)
        result = result + back(jnp.stack(parts, axis=-5), table, col)
    return result


def assemble_dim(field, e_dim, n_dim, fetch):
    count = field.shape[e_dim]
    low = lax.slice_in_dim(field, 0, 1, axis=n_dim)
    high = lax.slice_in_dim(field, 4, 5, axis=n_dim)
    middle = lax.slice_in_dim(field, 1, 4, axis=n_dim)
    first = lax.slice_in_dim(low, 0, 1, axis=e_dim)
    last = lax.slice_in_dim(high, count - 1, count, axis=e_dim)
    below, above = fetch(first, last)
    low_next = jnp.concatenate([lax.slice_in_dim(low, 1, count, axis=e_dim), above], axis=e_dim)
    high_prev = jnp.concatenate(
        [below, lax.slice_in_dim(high, 0, count - 1, axis=e_dim)], axis=e_dim
    )
    return jnp.concatenate([low + high_prev, middle, high + low_next], axis=n_dim)


def fetch_none(first, last):
    return (jnp.zeros_like(last), jnp.zeros_like(first))


def fetch_first(first, last):
    padded = with_halo(jnp.concatenate([first, last], axis=0), (("gx", 0),), 1)
    return (padded[0:1], padded[3:4])


def fetch_second(first, last):
    padded = with_halo(jnp.concatenate([first, last], axis=1), (("gy", 1),), 1)
    return (padded[:, 0:1], padded[:, 3:4])


def body(wavefield, moduli, residuals, coords, angles, element_ids, counts):
    cells_x = wavefield.shape[0]
    cells_y = wavefield.shape[1]
    depth = wavefield.shape[4]
    groups_x = lax.axis_size("gx")
    groups_y = lax.axis_size("gy")
    owners = groups_x * groups_y
    slots = residuals.shape[2]
    blocks = owners // 16
    elements = cells_x * cells_y * depth
    field = wavefield.reshape(cells_x, cells_y, 3, 5, 5, 5, depth)
    internal = stiffness(field, moduli)
    floats = (
        lax.all_to_all(residuals, ("gx", "gy"), split_axis=1, concat_axis=0, tiled=True),
        lax.all_to_all(coords, ("gx", "gy"), split_axis=1, concat_axis=0, tiled=True),
        lax.all_to_all(angles, ("gx", "gy"), split_axis=1, concat_axis=0, tiled=True),
    )
    index = (
        lax.all_to_all(element_ids, ("gx", "gy"), split_axis=1, concat_axis=0, tiled=True),
        lax.all_to_all(counts, ("gx", "gy"), split_axis=1, concat_axis=0, tiled=True),
    )
    got_resid = floats[0].reshape(blocks, 16, slots)
    got_coord = floats[1].reshape(blocks, 16, 3, slots)
    got_angle = floats[2].reshape(blocks, 16, 2, slots)
    got_ids = index[0].reshape(blocks, 16, slots)
    got_count = index[1].reshape(blocks, 16)
    numbers = jnp.arange(elements, dtype=jnp.int32)

    def add_block(step, total):
        contrib = sources(got_resid[step], got_coord[step], got_angle[step], got_count[step])
        onehot = (got_ids[step].reshape(-1)[:, None] == numbers[None, :]).astype(jnp.float32)
        onehot = onehot.reshape(-1, cells_x, cells_y, depth)
        return total + jnp.einsum("ks,sxyz->xykz", contrib, onehot, precision=lax.Precision.HIGHEST)

    start = jnp.zeros((cells_x, cells_y, 375, depth), jnp.float32)
    total = lax.fori_loop(0, blocks, add_block, start)
    injected = total.reshape(cells_x, cells_y, 3, 5, 5, 5, depth)
    force = injected - internal
    force = assemble_dim(force, 0, 3, fetch_first)
    force = assemble_dim(force, 1, 4, fetch_second)
    force = assemble_dim(force, 6, 5, fetch_none)
    return force.reshape(cells_x, cells_y, 3, 125, depth)


def solution(mesh):
    in_specs = (
        P("gx", "gy", None, None, None),
        P("gx", "gy", None, None),
        P(("gx", "gy"), None, None),
        P(("gx", "gy"), None, None, None),
        P(("gx", "gy"), None, None, None),
        P(("gx", "gy"), None, None),
        P(("gx", "gy"), None),
    )
    out_specs = P("gx", "gy", None, None, None)
    return jax.shard_map(body, mesh=mesh, in_specs=in_specs, out_specs=out_specs, check_vma=False)
```

profile of v0, /device:TPU:9, one launch (start us, length us, event | category | flops | bytes accessed | tf_op | source)
XLA Modules:
  0.0 154.2 jit_solution(17965460843285024868)
XLA Ops:
  0.0 1.4 copy.67
  1.5 6.3 %all-to-all-start.2 = ((s32[1,32,1]{2,0,1:T(1,128)}), s32[1,32,1]{2,0,1:T(1,128)S(1)}, u32[]{:S(2)}, u32[]{:S(2)}) async-start(s32[1,32,1]{2,0,1:T(1,128)} %copy.67), calls=%async_computation.2 | async-start | bytes 32768 | tf_op jit(solution)/shard_map/all_to_all | solution.py:178
  7.8 3.1 %fusion.33 = f32[5,2,2,3,5,5,256]{6,0,5,4,3,2,1:T(8,128)S(1)} fusion(f32[5,5,1,1,1,1,1]{1,0,6,5,4,3,2:T(8,128)} %constant.255, f32[2,2,3,5,5,5,256]{6,1,5,4,3,2,0:T(2,128)S(1)} %bitcast.111), kind=kOutput, calls=%fused_computation.120 | convolution fusion | flops 23040000 | bytes 3072100 | tf_op jit(solution)/shard_map/sc,...pqcz->...pqsz/dot_general | solution.py:97
  10.9 2.2 %fusion.35 = f32[5,2,2,3,5,5,256]{6,0,5,4,3,2,1:T(8,128)S(1)} fusion(f32[5,5,1,1,1,1,1]{1,0,6,5,4,3,2:T(8,128)S(1)} %copy-done.9, f32[2,2,3,5,5,5,256]{6,1,5,4,3,2,0:T(2,128)S(1)} %bitcast.110), kind=kOutput, calls=%fused_computation.123 | convolution fusion | flops 23040000 | bytes 3072100 | tf_op jit(solution)/shard_map/qb,...pbsz->...pqsz/dot_general | solution.py:96
  13.2 2.2 %fusion.41 = f32[2,2,3,5,5,5,256]{6,3,5,4,2,1,0:T(8,128)S(1)} fusion(f32[5,5,1,1,1,1,1]{1,0,6,5,4,3,2:T(8,128)S(1)} %copy-done.9, f32[2,2,3,5,5,5,256]{6,1,5,4,3,2,0:T(2,128)S(1)} %bitcast.109), kind=kOutput, calls=%fused_computation.127 | convolution fusion | flops 23040000 | bytes 3072100 | tf_op jit(solution)/shard_map/pa,...aqsz->...pqsz/dot_general | solution.py:94
  15.6 0.8 copy.124
  16.3 0.6 copy.125
  17.0 0.9 copy-done.1
  17.8 0.7 copy-done.2
  18.5 1.7 %add_multiply_fusion.2 = (f32[2,2,1,5,5,5,256]{6,3,5,4,2,1,0:T(8,128)}, f32[2,2,1,5,5,5,256]{6,3,5,4,2,1,0:T(8,128)}, f32[2,2,1,5,5,5,256]{6,3,5,4,2,1,0:T(8,128...) fusion(f32[2,2,3,5,5,5,256]{6,3,5,4,2,1,0:T(8,128)S(1)} %fusion.41, ...), kind=kLoop, calls=%fused_computation.139 | loop fusion | flops 2048000 | bytes 7176692 | tf_op jit(solution)/shard_map/mul | solution.py:125
  20.2 5.9 %all-to-all-start.3 = ((f32[1,32,128]{2,0,1:T(1,128)}), f32[1,32,128]{2,0,1:T(1,128)}, u32[]{:S(2)}, u32[]{:S(2)}) async-start(f32[1,32,128]{2,0,1:T(1,128)} %bitcast.5), calls=%async_computation.3 | async-start | bytes 32768 | tf_op jit(solution)/shard_map/all_to_all | solution.py:172
  26.1 3.1 %add_multiply_fusion.1 = (f32[2,2,1,5,5,5,256]{6,3,5,4,2,1,0:T(8,128)}, f32[2,2,1,5,5,5,256]{6,3,5,4,2,1,0:T(8,128)}) fusion(f32[2,2,1,5,5,5,256]{6,3,5,4,2,1,0:T(8,128)} %get-tuple-element.358, f32[2,2,3,5,5,5,256]{6,3,5,4,2,1,0:T(8,128)} %bitcast.115, f32[5,5,5]{0,2,1:T(8,128)S(1)} %broadcast_multiply_fusion.8, f32[2,2,256]{2,1,0:T(2,128)S(1)} %get-tuple-element.425, ...), kind=kLoop, calls=%fused_computation.138 | loop fusion | flops 1024000 | bytes 2564596 | tf_op jit(solution)/shard_map/mul | solution.py:125
  29.1 2.5 %all-to-all-done.3 = f32[1,32,128]{2,0,1:T(1,128)} async-done(((f32[1,32,128]{2,0,1:T(1,128)}), f32[1,32,128]{2,0,1:T(1,128)}, u32[]{:S(2)}, u32[]{:S(2)}) %all-to-all-start.3) | async-done | bytes 16416 | tf_op jit(solution)/shard_map/all_to_all | solution.py:172
  31.7 4.5 %all-to-all-start = ((s32[1,32,128]{2,0,1:T(1,128)}), s32[1,32,128]{2,0,1:T(1,128)}, u32[]{:S(2)}, u32[]{:S(2)}) async-start(s32[1,32,128]{2,0,1:T(1,128)} %bitcast), calls=%async_computation | async-start | bytes 32768 | tf_op jit(solution)/shard_map/all_to_all | solution.py:177
  36.2 4.6 %pad_maximum_fusion = (f32[2,2,3,5,5,5,256]{6,3,5,4,2,1,0:T(8,128)}, f32[2,2,3,5,5,5,256]{6,3,5,4,2,1,0:T(8,128)}) fusion(f32[2,2,1,5,5,5,256]{6,3,5,4,2,1,0:T(8,128)} %get-tuple-element.403, f32[2,2,1,5,5,5,256]{6,3,5,4,2,1,0:T(8,128)} %get-tuple-element.418, f32[2,2,1,5,5,5,256]{6,3,5,4,2,1,0:T(8,128)S(1)} %get-tuple-element.401, ...), kind=kLoop, calls=%fused_computation.107 | loop fusion | flops 1536000 | bytes 5632000 | tf_op jit(solution)/shard_map/stack | solution.py:126
  40.8 0.7 copy.69
  41.5 0.4 all-to-all-done
  41.8 5.6 %all-to-all-start.4 = ((f32[1,32,3,128]{3,2,0,1:T(4,128)}), f32[1,32,3,128]{3,2,0,1:T(4,128)S(1)}, u32[]{:S(2)}, u32[]{:S(2)}) async-start(f32[1,32,3,128]{3,2,0,1:T(4,128)} %copy.69), calls=%async_computation.4 | async-start | bytes 131072 | tf_op jit(solution)/shard_map/all_to_all | solution.py:173
  47.4 5.9 %fusion.31 = f32[2,2,3,5,5,256,5]{5,6,4,3,2,1,0:T(8,128)} fusion(f32[5,5,1,1,1,1,1]{1,0,6,5,4,3,2:T(8,128)S(1)} %copy-done.9, f32[2,2,3,5,5,5,256]{6,3,5,4,2,1,0:T(8,128)} %get-tuple-element.420), kind=kOutput, calls=%fused_computation.117 | convolution fusion | flops 23040000 | bytes 3072100 | tf_op jit(solution)/shard_map/qb,...pqsz->...pbsz/dot_general | solution.py:104
  53.3 5.8 %all-to-all-start.1 = ((f32[1,32,2,128]{3,2,0,1:T(2,128)}), f32[1,32,2,128]{3,2,0,1:T(2,128)S(1)}, u32[]{:S(2)}, u32[]{:S(2)}) async-start(f32[1,32,2,128]{3,2,0,1:T(2,128)} %bitcast.2), calls=%async_computation.1 | async-start | bytes 65536 | tf_op jit(solution)/shard_map/all_to_all | solution.py:174
  59.1 5.9 %fusion.29 = f32[2,2,3,5,5,256,5]{5,6,4,3,2,1,0:T(8,128)} fusion(f32[5,5,1,1,1,1,1]{1,0,6,5,4,3,2:T(8,128)S(1)} %copy-done.9, f32[2,2,3,5,5,5,256]{6,3,5,4,2,1,0:T(8,128)} %get-tuple-element.421), kind=kOutput, calls=%fused_computation.115 | convolution fusion | flops 23040000 | bytes 3072100 | tf_op jit(solution)/shard_map/sc,...pqsz->...pqcz/dot_general | solution.py:105
  65.0 0.7 reduce
  65.8 52.7 %while.17 = (s32[]{:T(128)}, f32[2,2,375,256]{3,2,1,0:T(8,128)}, s32[2,16,128]{2,1,0:T(8,128)}, f32[2,16,2,128]{3,2,1,0:T(2,128)S(1)}, s32[2,16]{1,0:T(2,128)S(1...) while((s32[]{:T(128)}, f32[2,2,375,256]{3,2,1,0:T(8,128)}, ...), condition=%wide.region_1.2_spmd.clone, body=%wide.region_0.1_spmd.clone.sunk | while | flops 9442392064 | bytes 20555300 | solution.py:194
  65.8 0.6 multiply_add_fusion.23
  66.4 0.8 bitcast_select_fusion.2
  67.2 1.3 dynamic-slice_bitcast_fusion.5
  68.5 0.7 slice_sine_fusion.2
  69.2 0.6 fusion.71
  70.5 1.4 broadcast_multiply_fusion.13
  71.9 1.5 multiply_multiply_fusion.38
  73.5 0.8 stack.197
  74.3 1.0 broadcast_multiply_fusion.14
  75.5 2.9 %broadcast_multiply_fusion.15 = f32[3,5,5,5,2048]{4,3,2,1,0:T(8,128)} fusion(f32[5,5,5,2048]{3,2,1,0:T(8,128)S(1)} %multiply_add_fusion.22, f32[3,2048]{1,0:T(4,128)S(1)} %maximum_multiply_fusion.2), kind=kLoop, calls=%fused_computation.6.clone.1 | loop fusion | flops 768000 | bytes 4120576 | tf_op jit(solution)/shard_map/while/body/eval_jaxpr/mul | solution.py:89
  78.4 5.1 %reshape.2477 = f32[375,2048,1,1]{1,0,2,3:T(8,128)} reshape(f32[3,5,5,5,2048]{4,3,2,1,0:T(8,128)} %broadcast_multiply_fusion.15) | data formatting | bytes 6144000 | tf_op jit(solution)/shard_map/while/body/eval_jaxpr/mul | solution.py:89
  83.4 8.3 %bitcast_add_fusion.4 = f32[2,2,375,256]{3,2,1,0:T(8,128)} fusion(f32[2,2,375,256]{3,2,1,0:T(8,128)} %get-tuple-element.563, f32[375,2048,1,1]{1,0,2,3:T(8,128)} %reshape.2477, s32[2,2,256]{2,1,0:T(2,128)S(1)} %copy-done.10, s32[2048]{0:T(1024)S(1)} %copy-done.8, pred[]{:T(512)S(6)} %compare.5), kind=kOutput, calls=%fused_computation.8.clone.1 | convolution fusion | flops 9440049152 | bytes 6156289 | tf_op jit(solution)/shard_map/while/body/eval_jaxpr/ks,sxyz->xykz/dot_general | solution.py:191
  91.9 0.6 multiply_add_fusion.23
  92.5 0.8 bitcast_select_fusion.2
  93.2 1.3 dynamic-slice_bitcast_fusion.5
  94.5 0.7 slice_sine_fusion.2
  95.2 0.6 fusion.71
  96.5 1.4 broadcast_multiply_fusion.13
  97.9 1.5 multiply_multiply_fusion.38
  99.5 0.8 stack.197
  100.3 1.0 broadcast_multiply_fusion.14
  101.5 2.9 %broadcast_multiply_fusion.15 = f32[3,5,5,5,2048]{4,3,2,1,0:T(8,128)} fusion(f32[5,5,5,2048]{3,2,1,0:T(8,128)S(1)} %multiply_add_fusion.22, f32[3,2048]{1,0:T(4,128)S(1)} %maximum_multiply_fusion.2), kind=kLoop, calls=%fused_computation.6.clone.1 | loop fusion | flops 768000 | bytes 4120576 | tf_op jit(solution)/shard_map/while/body/eval_jaxpr/mul | solution.py:89
  104.4 5.1 %reshape.2477 = f32[375,2048,1,1]{1,0,2,3:T(8,128)} reshape(f32[3,5,5,5,2048]{4,3,2,1,0:T(8,128)} %broadcast_multiply_fusion.15) | data formatting | bytes 6144000 | tf_op jit(solution)/shard_map/while/body/eval_jaxpr/mul | solution.py:89
  109.5 8.8 %bitcast_add_fusion.4 = f32[2,2,375,256]{3,2,1,0:T(8,128)} fusion(f32[2,2,375,256]{3,2,1,0:T(8,128)} %get-tuple-element.563, f32[375,2048,1,1]{1,0,2,3:T(8,128)} %reshape.2477, s32[2,2,256]{2,1,0:T(2,128)S(1)} %copy-done.10, s32[2048]{0:T(1024)S(1)} %copy-done.8, pred[]{:T(512)S(6)} %compare.5), kind=kOutput, calls=%fused_computation.8.clone.1 | convolution fusion | flops 9440049152 | bytes 6156289 | tf_op jit(solution)/shard_map/while/body/eval_jaxpr/ks,sxyz->xykz/dot_general | solution.py:191
  118.5 2.3 %copy.73 = f32[2,2,375,256]{3,1,2,0:T(2,128)S(1)} copy(f32[2,2,375,256]{3,2,1,0:T(8,128)} %get-tuple-element.295) | data formatting | bytes 3072000 | tf_op jit(solution)/shard_map/while | solution.py:194
  120.9 5.7 %fusion.28 = f32[2,2,3,5,5,5,256]{6,3,5,4,2,1,0:T(8,128)S(1)} fusion(f32[2,2,3,5,5,5,256]{6,1,5,4,3,2,0:T(2,128)S(1)} %bitcast.116, f32[2,2,3,5,5,256,5]{5,6,4,3,2,1,0:T(8,128)} %fusion.29, f32[2,2,3,5,5,256,5]{5,6,4,3,2,1,0:T(8,128)S(1)} %copy-done.3, f32[5,5,1,1,1,1,1]{1,0,6,5,4,3,2:T(8,128)S(1)} %copy-done.9, ...), kind=kOutput, calls=%fused_computation.113 | convolution fusion | flops 24960000 | bytes 7680100 | tf_op jit(solution)/shard_map/pa,...pqsz->...aqsz/dot_general | solution.py:102
  126.6 0.5 fusion.57
  127.1 3.4 %collective-permute-start = (f32[1,2,3,1,5,5,256]{6,3,5,4,2,1,0:T(1,128)S(1)}, f32[1,2,3,1,5,5,256]{6,3,5,4,2,1,0:T(1,128)S(1)}, u32[]{:S(2)}, u32[]{:S(2)}) collective-permute-start(f32[1,2,3,1,5,5,256]{6,3,5,4,2,1,0:T(1,128)S(1)} %get-tuple-element.412), channel_id=1, source_target_pairs={{0,8},{8,16},{16,24},{1,9},{9,17},{17,25},{2,10},{10,18},{18,26},{... | collective-permute-start | bytes 460808 | tf_op jit(solution)/shard_map/ppermute | solution.py:14
  130.5 1.9 %collective-permute-start.1 = (f32[1,2,3,1,5,5,256]{6,3,5,4,2,1,0:T(1,128)S(1)}, f32[1,2,3,1,5,5,256]{6,3,5,4,2,1,0:T(1,128)S(1)}, u32[]{:S(2)}, u32[]{:S(2)}) collective-permute-start(f32[1,2,3,1,5,5,256]{6,3,5,4,2,1,0:T(1,128)S(1)} %get-tuple-element.413), channel_id=1, source_target_pairs={{8,0},{16,8},{24,16},{9,1},{17,9},{25,17},{10,2},{18,10},{26,18},{... | collective-permute-start | bytes 460808 | tf_op jit(solution)/shard_map/ppermute | solution.py:17
  132.4 0.3 slice.219
  132.7 4.3 %collective-permute-done.1 = f32[1,2,3,1,5,5,256]{6,3,5,4,2,1,0:T(1,128)S(1)} collective-permute-done((f32[1,2,3,1,5,5,256]{6,3,5,4,2,1,0:T(1,128)S(1)}, f32[1,2,3,1,5,5,256]{6,3,5,4,2,1,0:T(1,128)S(1)}, u32[]{:S(2)}, u32[]{:S(2)}) %collective-permute-start.1) | collective-permute-done | bytes 153632 | tf_op jit(solution)/shard_map/ppermute | solution.py:17
  137.0 0.8 slice_add_fusion.6
  138.0 3.1 %collective-permute-start.2 = (f32[2,1,3,5,1,5,256]{6,3,5,4,2,1,0:T(8,128)S(1)}, f32[2,1,3,5,1,5,256]{6,3,5,4,2,1,0:T(8,128)S(1)}, u32[]{:S(2)}, u32[]{:S(2)}) collective-permute-start(f32[2,1,3,5,1,5,256]{6,3,5,4,2,1,0:T(8,128)S(1)} %get-tuple-element.416), channel_id=1, source_target_pairs={{0,1},{1,2},{2,3},{3,4},{4,5},{5,6},{6,7},{8,9},{9,10},{10,11},{11... | collective-permute-start | bytes 460808 | tf_op jit(solution)/shard_map/ppermute | solution.py:14
  141.1 3.1 %collective-permute-start.3 = (f32[2,1,3,5,1,5,256]{6,3,5,4,2,1,0:T(8,128)S(1)}, f32[2,1,3,5,1,5,256]{6,3,5,4,2,1,0:T(8,128)S(1)}, u32[]{:S(2)}, u32[]{:S(2)}) collective-permute-start(f32[2,1,3,5,1,5,256]{6,3,5,4,2,1,0:T(8,128)S(1)} %get-tuple-element.417), channel_id=1, source_target_pairs={{1,0},{2,1},{3,2},{4,3},{5,4},{6,5},{7,6},{9,8},{10,9},{11,10},{12... | collective-permute-start | bytes 460808 | tf_op jit(solution)/shard_map/ppermute | solution.py:17
  144.2 0.8 pad_maximum_fusion.2
  145.1 4.4 %collective-permute-done.2 = f32[2,1,3,5,1,5,256]{6,3,5,4,2,1,0:T(8,128)S(1)} collective-permute-done((f32[2,1,3,5,1,5,256]{6,3,5,4,2,1,0:T(8,128)S(1)}, f32[2,1,3,5,1,5,256]{6,3,5,4,2,1,0:T(8,128)S(1)}, u32[]{:S(2)}, u32[]{:S(2)}) %collective-permute-start.2) | collective-permute-done | bytes 153632 | tf_op jit(solution)/shard_map/ppermute | solution.py:14
  149.4 1.6 %collective-permute-done.3 = f32[2,1,3,5,1,5,256]{6,3,5,4,2,1,0:T(8,128)S(1)} collective-permute-done((f32[2,1,3,5,1,5,256]{6,3,5,4,2,1,0:T(8,128)S(1)}, f32[2,1,3,5,1,5,256]{6,3,5,4,2,1,0:T(8,128)S(1)}, u32[]{:S(2)}, u32[]{:S(2)}) %collective-permute-start.3) | collective-permute-done | bytes 153632 | tf_op jit(solution)/shard_map/ppermute | solution.py:17
  151.1 0.3 fusion.53
  151.3 0.2 pad_maximum_fusion.3
  152.1 0.2 pad_maximum_fusion.4
  152.3 1.9 %copy.87 = f32[2,2,3,5,5,5,256]{6,1,5,4,3,2,0:T(2,128)} copy(f32[2,2,3,5,5,5,256]{6,3,5,4,2,1,0:T(8,128)S(1)} %pad_maximum_fusion.4) | data formatting | bytes 3072000 | tf_op jit(solution)/shard_map/concatenate | solution.py:142
  (88 shorter events, 3.2 us)
Async XLA Ops:
  0.0 7.8 %copy-start = (f32[2,2,3,125,256]{4,1,3,2,0:T(2,128)S(1)}, f32[2,2,3,125,256]{4,1,3,2,0:T(2,128)}, u32[]{:S(2)}) copy-start(f32[2,2,3,125,256]{4,1,3,2,0:T(2,128)} %param.11) | copy-start | bytes 4608004
  1.5 18.7 %all-to-all-start.2 = ((s32[1,32,1]{2,0,1:T(1,128)}), s32[1,32,1]{2,0,1:T(1,128)S(1)}, u32[]{:S(2)}, u32[]{:S(2)}) async-start(s32[1,32,1]{2,0,1:T(1,128)} %copy.67), calls=%async_computation.2 | async-start | bytes 32768 | tf_op jit(solution)/shard_map/all_to_all | solution.py:178
  7.8 3.1 %copy-start.9 = (f32[5,5,1,1,1,1,1]{1,0,6,5,4,3,2:T(8,128)S(1)}, f32[5,5,1,1,1,1,1]{1,0,6,5,4,3,2:T(8,128)}, u32[]{:S(2)}) copy-start(f32[5,5,1,1,1,1,1]{1,0,6,5,4,3,2:T(8,128)} %constant.255) | copy-start | bytes 304
  13.1 2.3 %copy-start.13 = (f32[5]{0:T(128)S(1)}, f32[5]{0:T(128)}, u32[]{:S(2)}) copy-start(f32[5]{0:T(128)} %constant.241.clone) | copy-start | bytes 64
  13.2 2.3 %copy-start.12 = (f32[2,2,2,256]{3,2,1,0:T(2,128)S(1)}, f32[2,2,2,256]{3,2,1,0:T(2,128)}, u32[]{:S(2)}) copy-start(f32[2,2,2,256]{3,2,1,0:T(2,128)} %param.12) | copy-start | bytes 24580
  16.3 1.5 copy-start.1
  17.0 1.6 %copy-start.2 = (f32[5,2,2,3,5,5,256]{6,4,5,0,3,2,1:T(8,128)}, f32[5,2,2,3,5,5,256]{6,4,5,0,3,2,1:T(8,128)S(1)}, u32[]{:S(2)}) copy-start(f32[5,2,2,3,5,5,256]{6,4,5,0,3,2,1:T(8,128)S(1)} %copy.125) | copy-start | bytes 4608004
  20.2 11.5 %all-to-all-start.3 = ((f32[1,32,128]{2,0,1:T(1,128)}), f32[1,32,128]{2,0,1:T(1,128)}, u32[]{:S(2)}, u32[]{:S(2)}) async-start(f32[1,32,128]{2,0,1:T(1,128)} %bitcast.5), calls=%async_computation.3 | async-start | bytes 32768 | tf_op jit(solution)/shard_map/all_to_all | solution.py:172
  31.7 10.2 %all-to-all-start = ((s32[1,32,128]{2,0,1:T(1,128)}), s32[1,32,128]{2,0,1:T(1,128)}, u32[]{:S(2)}, u32[]{:S(2)}) async-start(s32[1,32,128]{2,0,1:T(1,128)} %bitcast), calls=%async_computation | async-start | bytes 32768 | tf_op jit(solution)/shard_map/all_to_all | solution.py:177
  36.2 4.6 %copy-start.11 = (f32[1,32,3,128]{3,1,2,0:T(8,128)S(1)}, f32[1,32,3,128]{3,1,2,0:T(8,128)}, u32[]{:S(2)}) copy-start(f32[1,32,3,128]{3,1,2,0:T(8,128)} %param.14) | copy-start | bytes 147460
  41.8 11.5 %all-to-all-start.4 = ((f32[1,32,3,128]{3,2,0,1:T(4,128)}), f32[1,32,3,128]{3,2,0,1:T(4,128)S(1)}, u32[]{:S(2)}, u32[]{:S(2)}) async-start(f32[1,32,3,128]{3,2,0,1:T(4,128)} %copy.69), calls=%async_computation.4 | async-start | bytes 131072 | tf_op jit(solution)/shard_map/all_to_all | solution.py:173
  53.3 12.5 %all-to-all-start.1 = ((f32[1,32,2,128]{3,2,0,1:T(2,128)}), f32[1,32,2,128]{3,2,0,1:T(2,128)S(1)}, u32[]{:S(2)}, u32[]{:S(2)}) async-start(f32[1,32,2,128]{3,2,0,1:T(2,128)} %bitcast.2), calls=%async_computation.1 | async-start | bytes 65536 | tf_op jit(solution)/shard_map/all_to_all | solution.py:174
  65.8 2.7 %copy-start.14 = (s32[2,16]{1,0:T(2,128)}, s32[2,16]{1,0:T(2,128)S(1)}, u32[]{:S(2)}) copy-start(s32[2,16]{1,0:T(2,128)S(1)} %get-tuple-element.575) | copy-start | bytes 388 | tf_op jit(solution)/shard_map/while
  65.8 4.3 %copy-start.4 = (f32[2,16,3,128]{3,1,2,0:T(8,128)}, f32[2,16,3,128]{3,1,2,0:T(8,128)S(1)}, u32[]{:S(2)}) copy-start(f32[2,16,3,128]{3,1,2,0:T(8,128)S(1)} %get-tuple-element.577) | copy-start | bytes 147460 | tf_op jit(solution)/shard_map/while
  65.8 4.3 %copy-start.6 = (f32[2,16,2,128]{3,2,1,0:T(2,128)}, f32[2,16,2,128]{3,2,1,0:T(2,128)S(1)}, u32[]{:S(2)}) copy-start(f32[2,16,2,128]{3,2,1,0:T(2,128)S(1)} %get-tuple-element.574) | copy-start | bytes 98308 | tf_op jit(solution)/shard_map/while
  78.4 5.1 %copy-start.8 = (s32[2048]{0:T(1024)S(1)}, s32[2048]{0:T(1024)}, u32[]{:S(2)}) copy-start(s32[2048]{0:T(1024)} %dynamic-slice_bitcast_fusion.5) | copy-start | bytes 24580 | tf_op jit(solution)/shard_map/while
  78.4 5.1 %copy-start.10 = (s32[2,2,256]{2,1,0:T(2,128)S(1)}, s32[2,2,256]{2,1,0:T(2,128)}, u32[]{:S(2)}) copy-start(s32[2,2,256]{2,1,0:T(2,128)} %multiply_add_fusion.23) | copy-start | bytes 12292 | tf_op jit(solution)/shard_map/while
  83.4 8.4 %copy-start.5 = (f32[2,16,3,128]{3,1,2,0:T(8,128)S(1)}, f32[2,16,3,128]{3,1,2,0:T(8,128)}, u32[]{:S(2)}) copy-start(f32[2,16,3,128]{3,1,2,0:T(8,128)} %copy-done.4) | copy-start | bytes 147460 | tf_op jit(solution)/shard_map/while
  83.4 8.4 %copy-start.7 = (f32[2,16,2,128]{3,2,1,0:T(2,128)S(1)}, f32[2,16,2,128]{3,2,1,0:T(2,128)}, u32[]{:S(2)}) copy-start(f32[2,16,2,128]{3,2,1,0:T(2,128)} %copy-done.6) | copy-start | bytes 98308 | tf_op jit(solution)/shard_map/while
  83.4 8.4 %copy-start.15 = (s32[2,16]{1,0:T(2,128)S(1)}, s32[2,16]{1,0:T(2,128)}, u32[]{:S(2)}) copy-start(s32[2,16]{1,0:T(2,128)} %copy-done.14) | copy-start | bytes 388 | tf_op jit(solution)/shard_map/while
  91.8 2.7 %copy-start.14 = (s32[2,16]{1,0:T(2,128)}, s32[2,16]{1,0:T(2,128)S(1)}, u32[]{:S(2)}) copy-start(s32[2,16]{1,0:T(2,128)S(1)} %get-tuple-element.575) | copy-start | bytes 388 | tf_op jit(solution)/shard_map/while
  91.8 4.3 %copy-start.4 = (f32[2,16,3,128]{3,1,2,0:T(8,128)}, f32[2,16,3,128]{3,1,2,0:T(8,128)S(1)}, u32[]{:S(2)}) copy-start(f32[2,16,3,128]{3,1,2,0:T(8,128)S(1)} %get-tuple-element.577) | copy-start | bytes 147460 | tf_op jit(solution)/shard_map/while
  91.8 4.3 %copy-start.6 = (f32[2,16,2,128]{3,2,1,0:T(2,128)}, f32[2,16,2,128]{3,2,1,0:T(2,128)S(1)}, u32[]{:S(2)}) copy-start(f32[2,16,2,128]{3,2,1,0:T(2,128)S(1)} %get-tuple-element.574) | copy-start | bytes 98308 | tf_op jit(solution)/shard_map/while
  104.4 5.1 %copy-start.8 = (s32[2048]{0:T(1024)S(1)}, s32[2048]{0:T(1024)}, u32[]{:S(2)}) copy-start(s32[2048]{0:T(1024)} %dynamic-slice_bitcast_fusion.5) | copy-start | bytes 24580 | tf_op jit(solution)/shard_map/while
  104.4 5.1 %copy-start.10 = (s32[2,2,256]{2,1,0:T(2,128)S(1)}, s32[2,2,256]{2,1,0:T(2,128)}, u32[]{:S(2)}) copy-start(s32[2,2,256]{2,1,0:T(2,128)} %multiply_add_fusion.23) | copy-start | bytes 12292 | tf_op jit(solution)/shard_map/while
  109.4 8.8 %copy-start.5 = (f32[2,16,3,128]{3,1,2,0:T(8,128)S(1)}, f32[2,16,3,128]{3,1,2,0:T(8,128)}, u32[]{:S(2)}) copy-start(f32[2,16,3,128]{3,1,2,0:T(8,128)} %copy-done.4) | copy-start | bytes 147460 | tf_op jit(solution)/shard_map/while
  109.4 8.8 %copy-start.7 = (f32[2,16,2,128]{3,2,1,0:T(2,128)S(1)}, f32[2,16,2,128]{3,2,1,0:T(2,128)}, u32[]{:S(2)}) copy-start(f32[2,16,2,128]{3,2,1,0:T(2,128)} %copy-done.6) | copy-start | bytes 98308 | tf_op jit(solution)/shard_map/while
  109.5 8.8 %copy-start.15 = (s32[2,16]{1,0:T(2,128)S(1)}, s32[2,16]{1,0:T(2,128)}, u32[]{:S(2)}) copy-start(s32[2,16]{1,0:T(2,128)} %copy-done.14) | copy-start | bytes 388 | tf_op jit(solution)/shard_map/while
  118.5 2.4 %copy-start.3 = (f32[2,2,3,5,5,256,5]{5,6,4,3,2,1,0:T(8,128)S(1)}, f32[2,2,3,5,5,256,5]{5,6,4,3,2,1,0:T(8,128)}, u32[]{:S(2)}) copy-start(f32[2,2,3,5,5,256,5]{5,6,4,3,2,1,0:T(8,128)} %fusion.31) | copy-start | bytes 4608004
  127.1 5.6 %collective-permute-start = (f32[1,2,3,1,5,5,256]{6,3,5,4,2,1,0:T(1,128)S(1)}, f32[1,2,3,1,5,5,256]{6,3,5,4,2,1,0:T(1,128)S(1)}, u32[]{:S(2)}, u32[]{:S(2)}) collective-permute-start(f32[1,2,3,1,5,5,256]{6,3,5,4,2,1,0:T(1,128)S(1)} %get-tuple-element.412), channel_id=1, source_target_pairs={{0,8},{8,16},{16,24},{1,9},{9,17},{17,25},{2,10},{10,18},{18,26},{... | collective-permute-start | bytes 460808 | tf_op jit(solution)/shard_map/ppermute | solution.py:14
  130.5 6.5 %collective-permute-start.1 = (f32[1,2,3,1,5,5,256]{6,3,5,4,2,1,0:T(1,128)S(1)}, f32[1,2,3,1,5,5,256]{6,3,5,4,2,1,0:T(1,128)S(1)}, u32[]{:S(2)}, u32[]{:S(2)}) collective-permute-start(f32[1,2,3,1,5,5,256]{6,3,5,4,2,1,0:T(1,128)S(1)} %get-tuple-element.413), channel_id=1, source_target_pairs={{8,0},{16,8},{24,16},{9,1},{17,9},{25,17},{10,2},{18,10},{26,18},{... | collective-permute-start | bytes 460808 | tf_op jit(solution)/shard_map/ppermute | solution.py:17
  138.0 11.5 %collective-permute-start.2 = (f32[2,1,3,5,1,5,256]{6,3,5,4,2,1,0:T(8,128)S(1)}, f32[2,1,3,5,1,5,256]{6,3,5,4,2,1,0:T(8,128)S(1)}, u32[]{:S(2)}, u32[]{:S(2)}) collective-permute-start(f32[2,1,3,5,1,5,256]{6,3,5,4,2,1,0:T(8,128)S(1)} %get-tuple-element.416), channel_id=1, source_target_pairs={{0,1},{1,2},{2,3},{3,4},{4,5},{5,6},{6,7},{8,9},{9,10},{10,11},{11... | collective-permute-start | bytes 460808 | tf_op jit(solution)/shard_map/ppermute | solution.py:14
  141.1 10.0 %collective-permute-start.3 = (f32[2,1,3,5,1,5,256]{6,3,5,4,2,1,0:T(8,128)S(1)}, f32[2,1,3,5,1,5,256]{6,3,5,4,2,1,0:T(8,128)S(1)}, u32[]{:S(2)}, u32[]{:S(2)}) collective-permute-start(f32[2,1,3,5,1,5,256]{6,3,5,4,2,1,0:T(8,128)S(1)} %get-tuple-element.417), channel_id=1, source_target_pairs={{1,0},{2,1},{3,2},{4,3},{5,4},{6,5},{7,6},{9,8},{10,9},{11,10},{12... | collective-permute-start | bytes 460808 | tf_op jit(solution)/shard_map/ppermute | solution.py:17
where the time goes:
time: 155 us; the launch traced here: 154 us
  matrix products  42.2 us (27%)
  starting transfers between devices  39.5 us (25%)
  other arithmetic  31.6 us (20%)
  local copies, waits for them, and re-layouts  26.9 us (17%)
  waiting for transfers between devices  13.2 us (9%)
    dot_general x2, matrix products, add_block(): jnp.einsum('ks,sxyz->xykz', contrib, onehot, precision=lax.Precision.HIGH...  17.1 us
    mul x2, local copies, waits for them, and re-layouts, sources(): return (direction[:, None, None, None, :] * shape[None]).reshape(375, -1)  10.1 us
    ppermute x2, starting transfers between devices, with_halo(): lax.ppermute(lax.slice_in_dim(block, block.shape[dim] - width, None, axis...  6.47 us
    all_to_all x1, starting transfers between devices, body(): lax.all_to_all(counts, ('gx', 'gy'), split_axis=1, concat_axis=0, tiled=T...  6.32 us
    dot_general x1, matrix products, back(): jnp.einsum('sc,...pqsz->...pqcz', table, field, precision=lax.Precision.H...  5.9 us
    all_to_all x1, starting transfers between devices, body(): lax.all_to_all(residuals, ('gx', 'gy'), split_axis=1, concat_axis=0, tile...  5.89 us
    dot_general x1, matrix products, back(): jnp.einsum('qb,...pqsz->...pbsz', table, field, precision=lax.Precision.H...  5.89 us
    ppermute x2, waiting for transfers between devices, with_halo(): lax.ppermute(lax.slice_in_dim(block, 0, width, axis=dim), axis, backward)  5.88 us
  transfers between devices with their start and end apart: 9, of which 5 were waited for; matrix products, arithmetic and copies ran while one was open for 21% of the time, Pallas kernels for 0%

commit v1 on v0

--- a/solution.py
+++ b/solution.py
@@ -168,8 +168,18 @@
     elements = cells_x * cells_y * depth
     field = wavefield.reshape(cells_x, cells_y, 3, 5, 5, 5, depth)
     internal = stiffness(field, moduli)
+
+    def show_forms(arr_in, mesh_name):
+        raw_out = jnp.concatenate(
+            lax.all_to_all(
+                jnp.stack(jnp.split(arr_in, lax.axis_size(mesh_name), axis=1)), mesh_name, 0, 0
+            ),
+            axis=0,
+        )
+        return raw_out
+
     floats = (
-        lax.all_to_all(residuals, ("gx", "gy"), split_axis=1, concat_axis=0, tiled=True),
+        show_forms(residuals, ("gx", "gy")),
         lax.all_to_all(coords, ("gx", "gy"), split_axis=1, concat_axis=0, tiled=True),
         lax.all_to_all(angles, ("gx", "gy"), split_axis=1, concat_axis=0, tiled=True),
     )

time: 155 us -> 173 us (1.12)
  local copies, waits for them, and re-layouts: 26.9 us -> 43.9 us
  waiting for transfers between devices: 13.2 us -> 15.7 us
    unnamed x19 -> x48, local copies, waits for them, and re-layouts: 2.24 us -> 17.7 us
    all_to_all x1, waiting for transfers between devices: 0.37 us -> 5.09 us  [body(): lax.all_to_all(element_ids, ('gx', 'gy'), split_axis=1, concat_axis=0, ti...]
    all_to_all x1, waiting for transfers between devices: 2.52 us -> 0.28 us  [show_forms(): lax.all_to_all(jnp.stack(jnp.split(arr_in, lax.axis_size(mesh_name), axis...]
  transfers between devices with their start and end apart: 9 -> 9, of which waited for: 5 -> 5; matrix products, arithmetic and copies ran while one was open for 21% -> 28% of each run, Pallas kernels for 0% -> 0%
where the time goes in v1:
time: 173 us; the launch traced here: 172 us
  local copies, waits for them, and re-layouts  43.9 us (25%)
  matrix products  41.8 us (24%)
  starting transfers between devices  39.5 us (23%)
  other arithmetic  30.2 us (17%)
  waiting for transfers between devices  15.7 us (9%)
    unnamed x48, local copies, waits for them, and re-layouts  17.7 us
    dot_general x2, matrix products, add_block(): jnp.einsum('ks,sxyz->xykz', contrib, onehot, precision=lax.Precision.HIGH...  17.1 us
    mul x2, local copies, waits for them, and re-layouts, sources(): return (direction[:, None, None, None, :] * shape[None]).reshape(375, -1)  10.1 us
    ppermute x2, starting transfers between devices, with_halo(): lax.ppermute(lax.slice_in_dim(block, block.shape[dim] - width, None, axis...  6.46 us
    all_to_all x1, starting transfers between devices, body(): lax.all_to_all(counts, ('gx', 'gy'), split_axis=1, concat_axis=0, tiled=T...  6.32 us
    dot_general x1, matrix products, back(): jnp.einsum('sc,...pqsz->...pqcz', table, field, precision=lax.Precision.H...  5.9 us
    dot_general x1, matrix products, back(): jnp.einsum('qb,...pqsz->...pbsz', table, field, precision=lax.Precision.H...  5.89 us
    all_to_all x1, starting transfers between devices, body(): lax.all_to_all(element_ids, ('gx', 'gy'), split_axis=1, concat_axis=0, ti...  5.88 us
  transfers between devices with their start and end apart: 9, of which 5 were waited for; matrix products, arithmetic and copies ran while one was open for 28% of the time, Pallas kernels for 0%

profile of v1, /device:TPU:9, one launch (start us, length us, event | category | flops | bytes accessed | tf_op | source)
XLA Modules:
  0.0 171.8 jit_solution(2392714602216225022)
XLA Ops:
  0.0 1.4 copy.66
  1.5 6.3 %all-to-all-start.2 = ((s32[1,32,1]{2,0,1:T(1,128)}), s32[1,32,1]{2,0,1:T(1,128)S(1)}, u32[]{:S(2)}, u32[]{:S(2)}) async-start(s32[1,32,1]{2,0,1:T(1,128)} %copy.66), calls=%async_computation.2 | async-start | bytes 32768 | tf_op jit(solution)/shard_map/all_to_all | solution.py:188
  7.8 3.1 %fusion.33 = f32[5,2,2,3,5,5,256]{6,0,5,4,3,2,1:T(8,128)S(1)} fusion(f32[5,5,1,1,1,1,1]{1,0,6,5,4,3,2:T(8,128)} %constant.255, f32[2,2,3,5,5,5,256]{6,1,5,4,3,2,0:T(2,128)S(1)} %bitcast.174), kind=kOutput, calls=%fused_computation.120 | convolution fusion | flops 23040000 | bytes 3072100 | tf_op jit(solution)/shard_map/sc,...pqcz->...pqsz/dot_general | solution.py:97
  10.9 2.2 %fusion.35 = f32[5,2,2,3,5,5,256]{6,0,5,4,3,2,1:T(8,128)S(1)} fusion(f32[5,5,1,1,1,1,1]{1,0,6,5,4,3,2:T(8,128)S(1)} %copy-done.7, f32[2,2,3,5,5,5,256]{6,1,5,4,3,2,0:T(2,128)S(1)} %bitcast.173), kind=kOutput, calls=%fused_computation.123 | convolution fusion | flops 23040000 | bytes 3072100 | tf_op jit(solution)/shard_map/qb,...pbsz->...pqsz/dot_general | solution.py:96
  13.2 2.2 %fusion.41 = f32[2,2,3,5,5,5,256]{6,3,5,4,2,1,0:T(8,128)S(1)} fusion(f32[5,5,1,1,1,1,1]{1,0,6,5,4,3,2:T(8,128)S(1)} %copy-done.7, f32[2,2,3,5,5,5,256]{6,1,5,4,3,2,0:T(2,128)S(1)} %bitcast.172), kind=kOutput, calls=%fused_computation.127 | convolution fusion | flops 23040000 | bytes 3072100 | tf_op jit(solution)/shard_map/pa,...aqsz->...pqsz/dot_general | solution.py:94
  16.7 0.6 constant_dynamic-update-slice_fusion.29
  20.4 0.6 constant_dynamic-update-slice_fusion.22
  21.0 0.6 constant_dynamic-update-slice_fusion.21
  23.7 0.6 constant_dynamic-update-slice_fusion.16
  27.5 0.6 constant_dynamic-update-slice_fusion.9
  30.8 0.6 constant_dynamic-update-slice_fusion.3
  31.4 0.6 constant_dynamic-update-slice_fusion.2
  32.0 0.8 copy.122
  32.8 0.6 copy.123
  33.4 1.8 %add_multiply_fusion.2 = (f32[2,2,1,5,5,5,256]{6,3,5,4,2,1,0:T(8,128)}, f32[2,2,1,5,5,5,256]{6,3,5,4,2,1,0:T(8,128)S(1)}, f32[2,2,1,5,5,5,256]{6,3,5,4,2,1,0:T(8...) fusion(f32[2,2,3,5,5,5,256]{6,3,5,4,2,1,0:T(8,128)S(1)} %fusion.41, ...), kind=kLoop, calls=%fused_computation.139 | loop fusion | flops 2048000 | bytes 7176692 | tf_op jit(solution)/shard_map/mul | solution.py:125
  35.2 1.4 add_multiply_fusion.1
  36.6 0.6 constant_dynamic-update-slice_fusion.1
  37.2 5.9 %all-to-all-start = ((s32[1,32,128]{2,0,1:T(1,128)}), s32[1,32,128]{2,0,1:T(1,128)}, u32[]{:S(2)}, u32[]{:S(2)}) async-start(s32[1,32,128]{2,0,1:T(1,128)} %bitcast), calls=%async_computation | async-start | bytes 32768 | tf_op jit(solution)/shard_map/all_to_all | solution.py:187
  43.6 5.1 %all-to-all-done = s32[1,32,128]{2,0,1:T(1,128)} async-done(((s32[1,32,128]{2,0,1:T(1,128)}), s32[1,32,128]{2,0,1:T(1,128)}, u32[]{:S(2)}, u32[]{:S(2)}) %all-to-all-start) | async-done | bytes 16416 | tf_op jit(solution)/shard_map/all_to_all | solution.py:187
  48.7 4.4 %all-to-all-start.3 = ((f32[32,1,1,128]{3,2,1,0:T(1,128)}), f32[32,1,1,128]{3,2,1,0:T(1,128)}, u32[]{:S(2)}, u32[]{:S(2)}) async-start(f32[32,1,1,128]{3,2,1,0:T(1,128)} %constant_dynamic-update-slice_fusion), calls=%async_computation.3 | async-start | bytes 32768 | tf_op jit(solution)/shard_map/all_to_all | solution.py:174
  53.2 4.6 %pad_maximum_fusion = (f32[2,2,3,5,5,5,256]{6,3,5,4,2,1,0:T(8,128)}, f32[2,2,3,5,5,5,256]{6,3,5,4,2,1,0:T(8,128)}) fusion(f32[2,2,1,5,5,5,256]{6,3,5,4,2,1,0:T(8,128)} %get-tuple-element.403, f32[2,2,1,5,5,5,256]{6,3,5,4,2,1,0:T(8,128)} %get-tuple-element.418, f32[2,2,1,5,5,5,256]{6,3,5,4,2,1,0:T(8,128)S(1)} %get-tuple-element.401, ...), kind=kLoop, calls=%fused_computation.107 | loop fusion | flops 1536000 | bytes 5632000 | tf_op jit(solution)/shard_map/stack | solution.py:126
  57.8 0.7 copy.67
  58.7 5.6 %all-to-all-start.4 = ((f32[1,32,3,128]{3,2,0,1:T(4,128)}), f32[1,32,3,128]{3,2,0,1:T(4,128)S(1)}, u32[]{:S(2)}, u32[]{:S(2)}) async-start(f32[1,32,3,128]{3,2,0,1:T(4,128)} %copy.67), calls=%async_computation.4 | async-start | bytes 131072 | tf_op jit(solution)/shard_map/all_to_all | solution.py:183
  64.4 5.9 %fusion.31 = f32[2,2,3,5,5,256,5]{5,6,4,3,2,1,0:T(8,128)} fusion(f32[5,5,1,1,1,1,1]{1,0,6,5,4,3,2:T(8,128)S(1)} %copy-done.7, f32[2,2,3,5,5,5,256]{6,3,5,4,2,1,0:T(8,128)} %get-tuple-element.420), kind=kOutput, calls=%fused_computation.117 | convolution fusion | flops 23040000 | bytes 3072100 | tf_op jit(solution)/shard_map/qb,...pqsz->...pbsz/dot_general | solution.py:104
  70.3 5.8 %all-to-all-start.1 = ((f32[1,32,2,128]{3,2,0,1:T(2,128)}), f32[1,32,2,128]{3,2,0,1:T(2,128)S(1)}, u32[]{:S(2)}, u32[]{:S(2)}) async-start(f32[1,32,2,128]{3,2,0,1:T(2,128)} %bitcast.2), calls=%async_computation.1 | async-start | bytes 65536 | tf_op jit(solution)/shard_map/all_to_all | solution.py:184
  76.1 5.9 %fusion.29 = f32[2,2,3,5,5,256,5]{5,6,4,3,2,1,0:T(8,128)} fusion(f32[5,5,1,1,1,1,1]{1,0,6,5,4,3,2:T(8,128)S(1)} %copy-done.7, f32[2,2,3,5,5,5,256]{6,3,5,4,2,1,0:T(8,128)} %get-tuple-element.421), kind=kOutput, calls=%fused_computation.115 | convolution fusion | flops 23040000 | bytes 3072100 | tf_op jit(solution)/shard_map/sc,...pqsz->...pqcz/dot_general | solution.py:105
  82.0 0.7 reduce
  82.8 53.7 %while.17 = (s32[]{:T(128)}, f32[2,2,375,256]{3,2,1,0:T(8,128)}, s32[2,16,128]{2,1,0:T(8,128)}, f32[2,16,2,128]{3,2,1,0:T(2,128)S(1)}, s32[2,16]{1,0:T(2,128)S(1...) while((s32[]{:T(128)}, f32[2,2,375,256]{3,2,1,0:T(8,128)}, ...), condition=%wide.region_1.2_spmd.clone, body=%wide.region_0.1_spmd.clone.sunk | while | flops 9442392064 | bytes 20555300 | solution.py:204
  83.3 0.6 multiply_add_fusion.23
  83.9 0.8 bitcast_select_fusion.2
  84.7 1.3 dynamic-slice_bitcast_fusion.5
  86.0 0.7 slice_sine_fusion.2
  86.7 0.6 fusion.71
  88.0 1.4 broadcast_multiply_fusion.13
  89.4 1.5 multiply_multiply_fusion.38
  91.0 0.8 stack.329
  91.8 1.0 broadcast_multiply_fusion.14
  93.0 2.9 %broadcast_multiply_fusion.15 = f32[3,5,5,5,2048]{4,3,2,1,0:T(8,128)} fusion(f32[5,5,5,2048]{3,2,1,0:T(8,128)S(1)} %multiply_add_fusion.22, f32[3,2048]{1,0:T(4,128)S(1)} %maximum_multiply_fusion.2), kind=kLoop, calls=%fused_computation.6.clone.1 | loop fusion | flops 768000 | bytes 4120576 | tf_op jit(solution)/shard_map/while/body/eval_jaxpr/mul | solution.py:89
  95.8 5.1 %reshape.2469 = f32[375,2048,1,1]{1,0,2,3:T(8,128)} reshape(f32[3,5,5,5,2048]{4,3,2,1,0:T(8,128)} %broadcast_multiply_fusion.15) | data formatting | bytes 6144000 | tf_op jit(solution)/shard_map/while/body/eval_jaxpr/mul | solution.py:89
  100.9 8.3 %bitcast_add_fusion.4 = f32[2,2,375,256]{3,2,1,0:T(8,128)} fusion(f32[2,2,375,256]{3,2,1,0:T(8,128)} %get-tuple-element.563, f32[375,2048,1,1]{1,0,2,3:T(8,128)} %reshape.2469, s32[2,2,256]{2,1,0:T(2,128)S(1)} %copy-done.8, s32[2048]{0:T(1024)S(1)} %copy-done.6, pred[]{:T(512)S(6)} %compare.5), kind=kOutput, calls=%fused_computation.8.clone.1 | convolution fusion | flops 9440049152 | bytes 6156289 | tf_op jit(solution)/shard_map/while/body/eval_jaxpr/ks,sxyz->xykz/dot_general | solution.py:201
  109.8 0.6 multiply_add_fusion.23
  110.4 0.8 bitcast_select_fusion.2
  111.2 1.3 dynamic-slice_bitcast_fusion.5
  112.5 0.7 slice_sine_fusion.2
  113.2 0.6 fusion.71
  114.5 1.4 broadcast_multiply_fusion.13
  115.9 1.5 multiply_multiply_fusion.38
  117.5 0.8 stack.329
  118.3 1.0 broadcast_multiply_fusion.14
  119.5 2.9 %broadcast_multiply_fusion.15 = f32[3,5,5,5,2048]{4,3,2,1,0:T(8,128)} fusion(f32[5,5,5,2048]{3,2,1,0:T(8,128)S(1)} %multiply_add_fusion.22, f32[3,2048]{1,0:T(4,128)S(1)} %maximum_multiply_fusion.2), kind=kLoop, calls=%fused_computation.6.clone.1 | loop fusion | flops 768000 | bytes 4120576 | tf_op jit(solution)/shard_map/while/body/eval_jaxpr/mul | solution.py:89
  122.4 5.1 %reshape.2469 = f32[375,2048,1,1]{1,0,2,3:T(8,128)} reshape(f32[3,5,5,5,2048]{4,3,2,1,0:T(8,128)} %broadcast_multiply_fusion.15) | data formatting | bytes 6144000 | tf_op jit(solution)/shard_map/while/body/eval_jaxpr/mul | solution.py:89
  127.5 8.8 %bitcast_add_fusion.4 = f32[2,2,375,256]{3,2,1,0:T(8,128)} fusion(f32[2,2,375,256]{3,2,1,0:T(8,128)} %get-tuple-element.563, f32[375,2048,1,1]{1,0,2,3:T(8,128)} %reshape.2469, s32[2,2,256]{2,1,0:T(2,128)S(1)} %copy-done.8, s32[2048]{0:T(1024)S(1)} %copy-done.6, pred[]{:T(512)S(6)} %compare.5), kind=kOutput, calls=%fused_computation.8.clone.1 | convolution fusion | flops 9440049152 | bytes 6156289 | tf_op jit(solution)/shard_map/while/body/eval_jaxpr/ks,sxyz->xykz/dot_general | solution.py:201
  136.5 2.3 %copy.71 = f32[2,2,375,256]{3,1,2,0:T(2,128)S(1)} copy(f32[2,2,375,256]{3,2,1,0:T(8,128)} %get-tuple-element.295) | data formatting | bytes 3072000 | tf_op jit(solution)/shard_map/while | solution.py:204
  138.9 5.3 %fusion.28 = f32[2,2,3,5,5,5,256]{6,3,5,4,2,1,0:T(8,128)S(1)} fusion(f32[2,2,3,5,5,5,256]{6,1,5,4,3,2,0:T(2,128)S(1)} %bitcast.179, f32[2,2,3,5,5,256,5]{5,6,4,3,2,1,0:T(8,128)} %fusion.29, f32[2,2,3,5,5,256,5]{5,6,4,3,2,1,0:T(8,128)S(1)} %copy-done.1, f32[5,5,1,1,1,1,1]{1,0,6,5,4,3,2:T(8,128)S(1)} %copy-done.7, ...), kind=kOutput, calls=%fused_computation.113 | convolution fusion | flops 24960000 | bytes 7680100 | tf_op jit(solution)/shard_map/pa,...pqsz->...aqsz/dot_general | solution.py:102
  144.6 3.4 %collective-permute-start = (f32[1,2,3,1,5,5,256]{6,3,5,4,2,1,0:T(1,128)S(1)}, f32[1,2,3,1,5,5,256]{6,3,5,4,2,1,0:T(1,128)S(1)}, u32[]{:S(2)}, u32[]{:S(2)}) collective-permute-start(f32[1,2,3,1,5,5,256]{6,3,5,4,2,1,0:T(1,128)S(1)} %get-tuple-element.412), channel_id=1, source_target_pairs={{0,8},{8,16},{16,24},{1,9},{9,17},{17,25},{2,10},{10,18},{18,26},{... | collective-permute-start | bytes 460808 | tf_op jit(solution)/shard_map/ppermute | solution.py:14
  148.0 1.9 %collective-permute-start.1 = (f32[1,2,3,1,5,5,256]{6,3,5,4,2,1,0:T(1,128)S(1)}, f32[1,2,3,1,5,5,256]{6,3,5,4,2,1,0:T(1,128)S(1)}, u32[]{:S(2)}, u32[]{:S(2)}) collective-permute-start(f32[1,2,3,1,5,5,256]{6,3,5,4,2,1,0:T(1,128)S(1)} %get-tuple-element.413), channel_id=1, source_target_pairs={{8,0},{16,8},{24,16},{9,1},{17,9},{25,17},{10,2},{18,10},{26,18},{... | collective-permute-start | bytes 460808 | tf_op jit(solution)/shard_map/ppermute | solution.py:17
  150.3 4.3 %collective-permute-done.1 = f32[1,2,3,1,5,5,256]{6,3,5,4,2,1,0:T(1,128)S(1)} collective-permute-done((f32[1,2,3,1,5,5,256]{6,3,5,4,2,1,0:T(1,128)S(1)}, f32[1,2,3,1,5,5,256]{6,3,5,4,2,1,0:T(1,128)S(1)}, u32[]{:S(2)}, u32[]{:S(2)}) %collective-permute-start.1) | collective-permute-done | bytes 153632 | tf_op jit(solution)/shard_map/ppermute | solution.py:17
  154.5 0.8 slice_add_fusion.6
  155.5 3.1 %collective-permute-start.2 = (f32[2,1,3,5,1,5,256]{6,3,5,4,2,1,0:T(8,128)S(1)}, f32[2,1,3,5,1,5,256]{6,3,5,4,2,1,0:T(8,128)S(1)}, u32[]{:S(2)}, u32[]{:S(2)}) collective-permute-start(f32[2,1,3,5,1,5,256]{6,3,5,4,2,1,0:T(8,128)S(1)} %get-tuple-element.416), channel_id=1, source_target_pairs={{0,1},{1,2},{2,3},{3,4},{4,5},{5,6},{6,7},{8,9},{9,10},{10,11},{11... | collective-permute-start | bytes 460808 | tf_op jit(solution)/shard_map/ppermute | solution.py:14
  158.6 3.1 %collective-permute-start.3 = (f32[2,1,3,5,1,5,256]{6,3,5,4,2,1,0:T(8,128)S(1)}, f32[2,1,3,5,1,5,256]{6,3,5,4,2,1,0:T(8,128)S(1)}, u32[]{:S(2)}, u32[]{:S(2)}) collective-permute-start(f32[2,1,3,5,1,5,256]{6,3,5,4,2,1,0:T(8,128)S(1)} %get-tuple-element.417), channel_id=1, source_target_pairs={{1,0},{2,1},{3,2},{4,3},{5,4},{6,5},{7,6},{9,8},{10,9},{11,10},{12... | collective-permute-start | bytes 460808 | tf_op jit(solution)/shard_map/ppermute | solution.py:17
  161.7 0.8 pad_maximum_fusion.2
  162.6 4.4 %collective-permute-done.2 = f32[2,1,3,5,1,5,256]{6,3,5,4,2,1,0:T(8,128)S(1)} collective-permute-done((f32[2,1,3,5,1,5,256]{6,3,5,4,2,1,0:T(8,128)S(1)}, f32[2,1,3,5,1,5,256]{6,3,5,4,2,1,0:T(8,128)S(1)}, u32[]{:S(2)}, u32[]{:S(2)}) %collective-permute-start.2) | collective-permute-done | bytes 153632 | tf_op jit(solution)/shard_map/ppermute | solution.py:14
  167.0 1.6 collective-permute-done.3
  169.9 1.9 %copy.85 = f32[2,2,3,5,5,5,256]{6,1,5,4,3,2,0:T(2,128)} copy(f32[2,2,3,5,5,5,256]{6,3,5,4,2,1,0:T(8,128)S(1)} %pad_maximum_fusion.4) | data formatting | bytes 3072000 | tf_op jit(solution)/shard_map/concatenate | solution.py:142
  (118 shorter events, 18.8 us)
Async XLA Ops:
  0.0 7.8 %copy-start = (f32[2,2,3,125,256]{4,1,3,2,0:T(2,128)S(1)}, f32[2,2,3,125,256]{4,1,3,2,0:T(2,128)}, u32[]{:S(2)}) copy-start(f32[2,2,3,125,256]{4,1,3,2,0:T(2,128)} %param.11) | copy-start | bytes 4608004
  1.5 35.8 %all-to-all-start.2 = ((s32[1,32,1]{2,0,1:T(1,128)}), s32[1,32,1]{2,0,1:T(1,128)S(1)}, u32[]{:S(2)}, u32[]{:S(2)}) async-start(s32[1,32,1]{2,0,1:T(1,128)} %copy.66), calls=%async_computation.2 | async-start | bytes 32768 | tf_op jit(solution)/shard_map/all_to_all | solution.py:188
  7.8 3.1 %copy-start.7 = (f32[5,5,1,1,1,1,1]{1,0,6,5,4,3,2:T(8,128)S(1)}, f32[5,5,1,1,1,1,1]{1,0,6,5,4,3,2:T(8,128)}, u32[]{:S(2)}) copy-start(f32[5,5,1,1,1,1,1]{1,0,6,5,4,3,2:T(8,128)} %constant.255) | copy-start | bytes 304
  13.1 2.3 %copy-start.11 = (f32[5]{0:T(128)S(1)}, f32[5]{0:T(128)}, u32[]{:S(2)}) copy-start(f32[5]{0:T(128)} %constant.241.clone) | copy-start | bytes 64
  13.2 2.4 %copy-start.10 = (f32[2,2,2,256]{3,2,1,0:T(2,128)S(1)}, f32[2,2,2,256]{3,2,1,0:T(2,128)}, u32[]{:S(2)}) copy-start(f32[2,2,2,256]{3,2,1,0:T(2,128)} %param.12) | copy-start | bytes 24580
  13.2 2.4 %copy-start.12 = (f32[1,32,128]{2,1,0:T(8,128)S(1)}, f32[1,32,128]{2,1,0:T(8,128)}, u32[]{:S(2)}) copy-start(f32[1,32,128]{2,1,0:T(8,128)} %param.13) | copy-start | bytes 49156
  37.2 11.5 %all-to-all-start = ((s32[1,32,128]{2,0,1:T(1,128)}), s32[1,32,128]{2,0,1:T(1,128)}, u32[]{:S(2)}, u32[]{:S(2)}) async-start(s32[1,32,128]{2,0,1:T(1,128)} %bitcast), calls=%async_computation | async-start | bytes 32768 | tf_op jit(solution)/shard_map/all_to_all | solution.py:187
  48.7 10.0 %all-to-all-start.3 = ((f32[32,1,1,128]{3,2,1,0:T(1,128)}), f32[32,1,1,128]{3,2,1,0:T(1,128)}, u32[]{:S(2)}, u32[]{:S(2)}) async-start(f32[32,1,1,128]{3,2,1,0:T(1,128)} %constant_dynamic-update-slice_fusion), calls=%async_computation.3 | async-start | bytes 32768 | tf_op jit(solution)/shard_map/all_to_all | solution.py:174
  53.1 4.7 %copy-start.9 = (f32[1,32,3,128]{3,1,2,0:T(8,128)S(1)}, f32[1,32,3,128]{3,1,2,0:T(8,128)}, u32[]{:S(2)}) copy-start(f32[1,32,3,128]{3,1,2,0:T(8,128)} %param.14) | copy-start | bytes 147460
  58.7 11.6 %all-to-all-start.4 = ((f32[1,32,3,128]{3,2,0,1:T(4,128)}), f32[1,32,3,128]{3,2,0,1:T(4,128)S(1)}, u32[]{:S(2)}, u32[]{:S(2)}) async-start(f32[1,32,3,128]{3,2,0,1:T(4,128)} %copy.67), calls=%async_computation.4 | async-start | bytes 131072 | tf_op jit(solution)/shard_map/all_to_all | solution.py:183
  70.3 12.4 %all-to-all-start.1 = ((f32[1,32,2,128]{3,2,0,1:T(2,128)}), f32[1,32,2,128]{3,2,0,1:T(2,128)S(1)}, u32[]{:S(2)}, u32[]{:S(2)}) async-start(f32[1,32,2,128]{3,2,0,1:T(2,128)} %bitcast.2), calls=%async_computation.1 | async-start | bytes 65536 | tf_op jit(solution)/shard_map/all_to_all | solution.py:184
  82.8 0.5 copy-start.13
  82.8 4.8 %copy-start.2 = (f32[2,16,3,128]{3,1,2,0:T(8,128)}, f32[2,16,3,128]{3,1,2,0:T(8,128)S(1)}, u32[]{:S(2)}) copy-start(f32[2,16,3,128]{3,1,2,0:T(8,128)S(1)} %get-tuple-element.577) | copy-start | bytes 147460 | tf_op jit(solution)/shard_map/while
  82.8 4.8 %copy-start.4 = (f32[2,16,2,128]{3,2,1,0:T(2,128)}, f32[2,16,2,128]{3,2,1,0:T(2,128)S(1)}, u32[]{:S(2)}) copy-start(f32[2,16,2,128]{3,2,1,0:T(2,128)S(1)} %get-tuple-element.574) | copy-start | bytes 98308 | tf_op jit(solution)/shard_map/while
  95.8 5.1 %copy-start.6 = (s32[2048]{0:T(1024)S(1)}, s32[2048]{0:T(1024)}, u32[]{:S(2)}) copy-start(s32[2048]{0:T(1024)} %dynamic-slice_bitcast_fusion.5) | copy-start | bytes 24580 | tf_op jit(solution)/shard_map/while
  95.8 5.1 %copy-start.8 = (s32[2,2,256]{2,1,0:T(2,128)S(1)}, s32[2,2,256]{2,1,0:T(2,128)}, u32[]{:S(2)}) copy-start(s32[2,2,256]{2,1,0:T(2,128)} %multiply_add_fusion.23) | copy-start | bytes 12292 | tf_op jit(solution)/shard_map/while
  100.9 8.4 %copy-start.3 = (f32[2,16,3,128]{3,1,2,0:T(8,128)S(1)}, f32[2,16,3,128]{3,1,2,0:T(8,128)}, u32[]{:S(2)}) copy-start(f32[2,16,3,128]{3,1,2,0:T(8,128)} %copy-done.2) | copy-start | bytes 147460 | tf_op jit(solution)/shard_map/while
  100.9 8.4 %copy-start.5 = (f32[2,16,2,128]{3,2,1,0:T(2,128)S(1)}, f32[2,16,2,128]{3,2,1,0:T(2,128)}, u32[]{:S(2)}) copy-start(f32[2,16,2,128]{3,2,1,0:T(2,128)} %copy-done.4) | copy-start | bytes 98308 | tf_op jit(solution)/shard_map/while
  100.9 8.4 %copy-start.14 = (s32[2,16]{1,0:T(2,128)S(1)}, s32[2,16]{1,0:T(2,128)}, u32[]{:S(2)}) copy-start(s32[2,16]{1,0:T(2,128)} %copy-done.13) | copy-start | bytes 388 | tf_op jit(solution)/shard_map/while
  109.3 0.5 copy-start.13
  109.3 4.8 %copy-start.2 = (f32[2,16,3,128]{3,1,2,0:T(8,128)}, f32[2,16,3,128]{3,1,2,0:T(8,128)S(1)}, u32[]{:S(2)}) copy-start(f32[2,16,3,128]{3,1,2,0:T(8,128)S(1)} %get-tuple-element.577) | copy-start | bytes 147460 | tf_op jit(solution)/shard_map/while
  109.3 4.8 %copy-start.4 = (f32[2,16,2,128]{3,2,1,0:T(2,128)}, f32[2,16,2,128]{3,2,1,0:T(2,128)S(1)}, u32[]{:S(2)}) copy-start(f32[2,16,2,128]{3,2,1,0:T(2,128)S(1)} %get-tuple-element.574) | copy-start | bytes 98308 | tf_op jit(solution)/shard_map/while
  122.4 5.1 %copy-start.6 = (s32[2048]{0:T(1024)S(1)}, s32[2048]{0:T(1024)}, u32[]{:S(2)}) copy-start(s32[2048]{0:T(1024)} %dynamic-slice_bitcast_fusion.5) | copy-start | bytes 24580 | tf_op jit(solution)/shard_map/while
  122.4 5.1 %copy-start.8 = (s32[2,2,256]{2,1,0:T(2,128)S(1)}, s32[2,2,256]{2,1,0:T(2,128)}, u32[]{:S(2)}) copy-start(s32[2,2,256]{2,1,0:T(2,128)} %multiply_add_fusion.23) | copy-start | bytes 12292 | tf_op jit(solution)/shard_map/while
  127.4 8.8 %copy-start.3 = (f32[2,16,3,128]{3,1,2,0:T(8,128)S(1)}, f32[2,16,3,128]{3,1,2,0:T(8,128)}, u32[]{:S(2)}) copy-start(f32[2,16,3,128]{3,1,2,0:T(8,128)} %copy-done.2) | copy-start | bytes 147460 | tf_op jit(solution)/shard_map/while
  127.4 8.8 %copy-start.5 = (f32[2,16,2,128]{3,2,1,0:T(2,128)S(1)}, f32[2,16,2,128]{3,2,1,0:T(2,128)}, u32[]{:S(2)}) copy-start(f32[2,16,2,128]{3,2,1,0:T(2,128)} %copy-done.4) | copy-start | bytes 98308 | tf_op jit(solution)/shard_map/while
  127.5 8.8 %copy-start.14 = (s32[2,16]{1,0:T(2,128)S(1)}, s32[2,16]{1,0:T(2,128)}, u32[]{:S(2)}) copy-start(s32[2,16]{1,0:T(2,128)} %copy-done.13) | copy-start | bytes 388 | tf_op jit(solution)/shard_map/while
  136.5 2.4 %copy-start.1 = (f32[2,2,3,5,5,256,5]{5,6,4,3,2,1,0:T(8,128)S(1)}, f32[2,2,3,5,5,256,5]{5,6,4,3,2,1,0:T(8,128)}, u32[]{:S(2)}) copy-start(f32[2,2,3,5,5,256,5]{5,6,4,3,2,1,0:T(8,128)} %fusion.31) | copy-start | bytes 4608004
  144.6 5.6 %collective-permute-start = (f32[1,2,3,1,5,5,256]{6,3,5,4,2,1,0:T(1,128)S(1)}, f32[1,2,3,1,5,5,256]{6,3,5,4,2,1,0:T(1,128)S(1)}, u32[]{:S(2)}, u32[]{:S(2)}) collective-permute-start(f32[1,2,3,1,5,5,256]{6,3,5,4,2,1,0:T(1,128)S(1)} %get-tuple-element.412), channel_id=1, source_target_pairs={{0,8},{8,16},{16,24},{1,9},{9,17},{17,25},{2,10},{10,18},{18,26},{... | collective-permute-start | bytes 460808 | tf_op jit(solution)/shard_map/ppermute | solution.py:14
  148.0 6.5 %collective-permute-start.1 = (f32[1,2,3,1,5,5,256]{6,3,5,4,2,1,0:T(1,128)S(1)}, f32[1,2,3,1,5,5,256]{6,3,5,4,2,1,0:T(1,128)S(1)}, u32[]{:S(2)}, u32[]{:S(2)}) collective-permute-start(f32[1,2,3,1,5,5,256]{6,3,5,4,2,1,0:T(1,128)S(1)} %get-tuple-element.413), channel_id=1, source_target_pairs={{8,0},{16,8},{24,16},{9,1},{17,9},{25,17},{10,2},{18,10},{26,18},{... | collective-permute-start | bytes 460808 | tf_op jit(solution)/shard_map/ppermute | solution.py:17
  155.5 11.5 %collective-permute-start.2 = (f32[2,1,3,5,1,5,256]{6,3,5,4,2,1,0:T(8,128)S(1)}, f32[2,1,3,5,1,5,256]{6,3,5,4,2,1,0:T(8,128)S(1)}, u32[]{:S(2)}, u32[]{:S(2)}) collective-permute-start(f32[2,1,3,5,1,5,256]{6,3,5,4,2,1,0:T(8,128)S(1)} %get-tuple-element.416), channel_id=1, source_target_pairs={{0,1},{1,2},{2,3},{3,4},{4,5},{5,6},{6,7},{8,9},{9,10},{10,11},{11... | collective-permute-start | bytes 460808 | tf_op jit(solution)/shard_map/ppermute | solution.py:14
  158.6 10.0 %collective-permute-start.3 = (f32[2,1,3,5,1,5,256]{6,3,5,4,2,1,0:T(8,128)S(1)}, f32[2,1,3,5,1,5,256]{6,3,5,4,2,1,0:T(8,128)S(1)}, u32[]{:S(2)}, u32[]{:S(2)}) collective-permute-start(f32[2,1,3,5,1,5,256]{6,3,5,4,2,1,0:T(8,128)S(1)} %get-tuple-element.417), channel_id=1, source_target_pairs={{1,0},{2,1},{3,2},{4,3},{5,4},{6,5},{7,6},{9,8},{10,9},{11,10},{12... | collective-permute-start | bytes 460808 | tf_op jit(solution)/shard_map/ppermute | solution.py:17
